TPU v7x, 512 devices: a whole 4x8x8 slice. The times are simulated.
512 devices in a mesh: gx: 64 (over z_hi, y, core), gy: 8 (over z_lo, x).
Axes of the slice: x: 4, y: 8, z: 8 (z_hi: 4, z_lo: 2; z = z_hi * 2 + z_lo), core: 2. Of those that a mesh axis runs over, the one named last changes fastest.
Arguments:
- field: bfloat16 [1, 512, 512, 128], P(None, 'gx', 'gy'), may hold values from -6 to 6
- conv_weight: bfloat16 [3, 3, 128, 128], replicated, may hold values from -0.1875 to 0.1875
- qkv_weight: bfloat16 [128, 384], replicated, may hold values from -4 to 4
- out_weight: bfloat16 [128, 128], replicated, may hold values from -0.5 to 0.5
Outputs:
- result: bfloat16 [1, 512, 512, 128], P(None, 'gx', 'gy')
All inputs are finite; a program needn't handle non-finite values.
Results may differ from a plain program's by a relative error of at most 0.0064.
Values may be sent and summed in bfloat16 or wider, within the bound.
No kernel may reach another device: no remote copies, remote signals or barrier semaphores. Data moves between devices by JAX's collectives and lax.ppermute only.
A program may use at most 64 MiB of HBM per device.

v0:
```python
import jax
import jax.numpy as jnp
from jax import lax
from jax.sharding import PartitionSpec as P

HEADS = 4
HEAD = 32


def padded_2(cells, sides, width):
    for axis, dim in sides:
        count = lax.axis_size(axis)
        head = lax.slice_in_dim(cells, 0, width, axis=dim)
        tail = lax.slice_in_dim(cells, cells.shape[dim] - width, cells.shape[dim], axis=dim)
        cells = jnp.concatenate(
            [
                lax.ppermute(tail, axis, [(i, (i + 1) % count) for i in range(count)]),
                cells,
                lax.ppermute(head, axis, [((i + 1) % count, i) for i in range(count)]),
            ],
            axis=dim,
        )
    return cells


def head_attend(parts):
    query, keyed, valued = parts
    scores = jnp.einsum("zqyd,zkyd->zyqk", query, keyed, preferred_element_type=jnp.float32)
    scores = scores / jnp.sqrt(jnp.float32(HEAD))
    top = jnp.max(scores, axis=-1, keepdims=True)
    expo = jnp.exp(scores - top)
    probs = (expo / jnp.sum(expo, axis=-1, keepdims=True)).astype(jnp.bfloat16)
    mixed = jnp.einsum("zyqk,zkyd->zqyd", probs, valued, preferred_element_type=jnp.float32)
    return mixed.astype(jnp.bfloat16)


def split_heads(block):
    planes, length, cols, width = block.shape
    return jnp.moveaxis(block.reshape(planes, length, cols, HEADS, width // HEADS), 3, 0)


def attend_lines(normed, qkv_weight):
    planes, length, cols, width = normed.shape
    qkv = jnp.dot(normed.reshape(-1, width), qkv_weight, preferred_element_type=jnp.float32)
    qkv = qkv.astype(jnp.bfloat16).reshape(planes, length, cols, 3 * width)
    query = split_heads(qkv[..., :width])
    keyed = split_heads(qkv[..., width : 2 * width])
    valued = split_heads(qkv[..., 2 * width :])
    mixed = lax.map(head_attend, (query, keyed, valued))
    return jnp.moveaxis(mixed, 0, 3).reshape(planes, length, cols, width)


def return_cells(block):
    return lax.all_to_all(block, "gx", split_axis=1, concat_axis=2, tiled=True)


def convolve(padded, conv_weight, rows, cols):
    planes = padded.shape[0]
    width = padded.shape[3]
    stem = jnp.zeros((planes, rows, cols, width), jnp.float32)
    for a in range(3):
        for b in range(3):
            window = padded[:, a : a + rows, b : b + cols, :]
            part = jnp.dot(
                window.reshape(-1, width), conv_weight[a, b], preferred_element_type=jnp.float32
            )
            stem = stem + part.reshape(planes, rows, cols, width)
    return stem


def normalize(stem):
    mean = jnp.mean(stem, axis=-1, keepdims=True)
    varia = jnp.mean((stem - mean) ** 2, axis=-1, keepdims=True)
    return ((stem - mean) / jnp.sqrt(varia + 1e-05)).astype(jnp.bfloat16)


def finish(stem, attended, out_weight):
    width = stem.shape[3]
    projected = jnp.dot(attended.reshape(-1, width), out_weight, preferred_element_type=jnp.float32)
    return (stem + projected.reshape(stem.shape)).astype(jnp.bfloat16)


def on_device(field, conv_weight, qkv_weight, out_weight):
    planes, rows, cols, width = field.shape
    padded = padded_2(field, (("gx", 1), ("gy", 2)), 1)
    stem = convolve(padded, conv_weight, rows, cols)
    normed = normalize(stem)
    attended = return_cells(
        attend_lines(
            lax.all_to_all(normed, "gx", split_axis=2, concat_axis=1, tiled=True), qkv_weight
        )
    )
    return finish(stem, attended, out_weight)


def solution(mesh):
    placed = (P(None, "gx", "gy", None), P(), P(), P())
    return jax.shard_map(
        on_device, mesh=mesh, in_specs=placed, out_specs=P(None, "gx", "gy", None), check_vma=False
    )
```

profile of v0, /device:TPU:7, one launch (start us, length us, event | category | flops | bytes accessed | tf_op | source)
XLA Modules:
  0.0 76.4 jit_solution(8873037923194557447)
XLA Ops:
  0.0 0.8 %fusion.78 = (bf16[1,1,64,128]{3,2,1,0:T(8,128)(2,1)S(1)}, bf16[1,1,64,128]{3,2,1,0:T(8,128)(2,1)S(1)}) fusion(bf16[1,8,64,128]{3,2,1,0:T(8,128)(2,1)} %param.6), kind=kLoop, calls=%fused_computation.102 | loop fusion | bytes 65536 | tf_op jit(solution)/shard_map/slice | solution.py:13
  0.8 3.8 %collective-permute-start = (bf16[1,1,64,128]{3,2,1,0:T(8,128)(2,1)S(1)}, bf16[1,1,64,128]{3,2,1,0:T(8,128)(2,1)S(1)}, u32[]{:S(2)}, u32[]{:S(2)}) collective-permute-start(bf16[1,1,64,128]{3,2,1,0:T(8,128)(2,1)S(1)} %get-tuple-element.51), channel_id=1, source_target_pairs={{0,8},{8,16},{16,24},{24,32},{32,40},{40,48},{48,56},{56,64},{64,7... | collective-permute-start | bytes 49160 | tf_op jit(solution)/shard_map/ppermute | solution.py:17
  4.5 1.9 %collective-permute-start.1 = (bf16[1,1,64,128]{3,2,1,0:T(8,128)(2,1)S(1)}, bf16[1,1,64,128]{3,2,1,0:T(8,128)(2,1)S(1)}, u32[]{:S(2)}, u32[]{:S(2)}) collective-permute-start(bf16[1,1,64,128]{3,2,1,0:T(8,128)(2,1)S(1)} %get-tuple-element.50), channel_id=1, source_target_pairs={{8,0},{16,8},{24,16},{32,24},{40,32},{48,40},{56,48},{64,56},{72,6... | collective-permute-start | bytes 49160 | tf_op jit(solution)/shard_map/ppermute | solution.py:19
  6.5 1.0 %constant_dynamic-update-slice_fusion.1 = bf16[1,10,64,128]{3,2,1,0:T(8,128)(2,1)S(1)} fusion(bf16[1,10,64,128]{3,2,1,0:T(8,128)(2,1)S(1)} %constant_dynamic-update-slice_fusion.2, bf16[1,8,64,128]{3,2,1,0:T(8,128)(2,1)} %param.6), kind=kLoop, calls=%fused_computation.87 | loop fusion | bytes 262144
  7.5 2.1 %collective-permute-done.1 = bf16[1,1,64,128]{3,2,1,0:T(8,128)(2,1)S(1)} collective-permute-done((bf16[1,1,64,128]{3,2,1,0:T(8,128)(2,1)S(1)}, bf16[1,1,64,128]{3,2,1,0:T(8,128)(2,1)S(1)}, u32[]{:S(2)}, u32[]{:S(2)}) %collective-permute-start.1) | collective-permute-done | bytes 16416 | tf_op jit(solution)/shard_map/ppermute | solution.py:19
  9.6 3.9 %collective-permute-start.2 = (bf16[1,10,1,128]{3,2,1,0:T(2,128)(2,1)S(1)}, bf16[1,10,1,128]{3,2,1,0:T(2,128)(2,1)S(1)}, u32[]{:S(2)}, u32[]{:S(2)}) collective-permute-start(bf16[1,10,1,128]{3,2,1,0:T(2,128)(2,1)S(1)} %get-tuple-element.48), channel_id=1, source_target_pairs={{0,1},{1,2},{2,3},{3,4},{4,5},{5,6},{6,7},{7,0},{8,9},{9,10},{10,1... | collective-permute-start | bytes 7688 | tf_op jit(solution)/shard_map/ppermute | solution.py:17
  13.5 1.9 %collective-permute-start.3 = (bf16[1,10,1,128]{3,2,1,0:T(2,128)(2,1)S(1)}, bf16[1,10,1,128]{3,2,1,0:T(2,128)(2,1)S(1)}, u32[]{:S(2)}, u32[]{:S(2)}) collective-permute-start(bf16[1,10,1,128]{3,2,1,0:T(2,128)(2,1)S(1)} %get-tuple-element.49), channel_id=1, source_target_pairs={{1,0},{2,1},{3,2},{4,3},{5,4},{6,5},{7,6},{0,7},{9,8},{10,9},{11,1... | collective-permute-start | bytes 7688 | tf_op jit(solution)/shard_map/ppermute | solution.py:19
  15.5 0.9 %fusion.40 = f32[8,64,128]{2,1,0:T(8,128)S(1)} fusion(bf16[1,8,64,128]{3,2,1,0:T(8,128)(2,1)S(1)} %copy-done.1, bf16[1,1,64,128]{3,2,1,0:T(8,128)(2,1)S(1)} %collective-permute-done, bf16[3,3,128,128]{3,2,1,0:T(8,128)(2,1)} %param.7), kind=kOutput, calls=%fused_computation.59 | convolution fusion | flops 16842752 | bytes 442368 | tf_op jit(solution)/shard_map/dot_general | solution.py:64
  16.8 3.2 %collective-permute-done.3 = bf16[1,10,1,128]{3,2,1,0:T(2,128)(2,1)S(1)} collective-permute-done((bf16[1,10,1,128]{3,2,1,0:T(2,128)(2,1)S(1)}, bf16[1,10,1,128]{3,2,1,0:T(2,128)(2,1)S(1)}, u32[]{:S(2)}, u32[]{:S(2)}) %collective-permute-start.3) | collective-permute-done | bytes 2592 | tf_op jit(solution)/shard_map/ppermute | solution.py:19
  20.9 0.3 fusion.79
  21.2 0.3 multiply_reduce_fusion
  21.5 0.2 fusion.47
  21.7 0.7 copy.21
  22.5 16.7 %all-to-all-start = ((bf16[1,8,64,128]{3,1,0,2:T(8,128)(2,1)}), bf16[1,8,64,128]{3,1,0,2:T(8,128)(2,1)S(1)}, u32[]{:S(2)}, u32[]{:S(2)}) async-start(bf16[1,8,64,128]{3,1,0,2:T(8,128)(2,1)} %copy.21), calls=%async_computation | async-start | bytes 262144 | tf_op jit(solution)/shard_map/all_to_all | solution.py:90
  39.2 12.8 %all-to-all-done = bf16[1,8,64,128]{3,1,0,2:T(8,128)(2,1)S(1)} async-done(((bf16[1,8,64,128]{3,1,0,2:T(8,128)(2,1)}), bf16[1,8,64,128]{3,1,0,2:T(8,128)(2,1)S(1)}, u32[]{:S(2)}, u32[]{:S(2)}) %all-to-all-start) | async-done | bytes 131104 | tf_op jit(solution)/shard_map/all_to_all | solution.py:90
  51.9 0.3 fusion.11
  52.3 3.4 %while.10 = (s32[]{:T(128)}, bf16[4,1,512,1,32]{2,4,3,1,0:T(8,128)(2,1)S(1)}, bf16[4,1,512,1,32]{2,4,3,1,0:T(8,128)(2,1)S(1)}, bf16[4,1,512,1,32]{2,4,3,1,0:T(8,...) while((s32[]{:T(128)}, bf16[4,1,512,1,32]{2,4,3,1,0:T(8,128)(2,1)S(1)}, ...), condition=%wide.region_5.6_spmd, body=%wide.region_2.5_spmd.sunk | while | flops 35404800 | bytes 3289157 | solution.py:49
  52.3 0.4 fusion.86
  52.7 0.2 fusion.87
  52.8 0.3 fusion.88
  53.1 0.4 fusion.86
  53.5 0.2 fusion.87
  53.7 0.3 fusion.88
  54.0 0.4 fusion.86
  54.6 0.3 fusion.88
  54.9 0.4 fusion.86
  55.4 0.3 fusion.88
  55.9 0.5 broadcast.39
  56.4 1.4 %reduce.8 = bf16[512,128]{1,0:T(8,128)(2,1)S(1)} reduce(bf16[512,1,1,128]{3,2,1,0:T(2,128)(2,1)S(1)} %bitcast.152, bf16[]{:T(256)} %broadcast.39), dimensions={1,2}, to_apply=%bitcast.132.reduce_sub_computation | reduce | bytes 262146
  57.9 16.8 %all_to_all.30 = bf16[64,2,512]{2,1,0:T(2,128)(2,1)S(1)} all-to-all(bf16[64,2,512]{2,1,0:T(2,128)(2,1)S(1)} %reshape.154), channel_id=1, replica_groups=mesh['gx'=64,'gy'=8] {'gx'}, dimensions={0} | all-to-all | bytes 262144 | tf_op jit(solution)/shard_map/all_to_all | solution.py:54
  74.9 0.7 copy-done.3
  75.6 0.8 %fusion.15 = bf16[1,8,64,128]{3,2,1,0:T(8,128)(2,1)} fusion(f32[8,64,128]{2,1,0:T(8,128)S(1)} %get-tuple-element.53, bf16[1,64,8,1,128]{4,2,1,3,0:T(8,128)(2,1)S(1)} %bitcast.156, bf16[128,128]{1,0:T(8,128)(2,1)S(1)} %copy-done.3), kind=kOutput, calls=%fused_computation.27 | convolution fusion | flops 16908288 | bytes 557056 | tf_op jit(solution)/shard_map/dot_general | solution.py:79
  (29 shorter events, 2.0 us)
Async XLA Ops:
  0.0 51.9 %copy-start = (bf16[128,384]{1,0:T(8,128)(2,1)S(1)}, bf16[128,384]{1,0:T(8,128)(2,1)}, u32[]{:S(2)}) copy-start(bf16[128,384]{1,0:T(8,128)(2,1)} %param.8) | copy-start | bytes 294916
  0.8 5.7 %collective-permute-start = (bf16[1,1,64,128]{3,2,1,0:T(8,128)(2,1)S(1)}, bf16[1,1,64,128]{3,2,1,0:T(8,128)(2,1)S(1)}, u32[]{:S(2)}, u32[]{:S(2)}) collective-permute-start(bf16[1,1,64,128]{3,2,1,0:T(8,128)(2,1)S(1)} %get-tuple-element.51), channel_id=1, source_target_pairs={{0,8},{8,16},{16,24},{24,32},{32,40},{40,48},{48,56},{56,64},{64,7... | collective-permute-start | bytes 49160 | tf_op jit(solution)/shard_map/ppermute | solution.py:17
  4.5 5.1 %collective-permute-start.1 = (bf16[1,1,64,128]{3,2,1,0:T(8,128)(2,1)S(1)}, bf16[1,1,64,128]{3,2,1,0:T(8,128)(2,1)S(1)}, u32[]{:S(2)}, u32[]{:S(2)}) collective-permute-start(bf16[1,1,64,128]{3,2,1,0:T(8,128)(2,1)S(1)} %get-tuple-element.50), channel_id=1, source_target_pairs={{8,0},{16,8},{24,16},{32,24},{40,32},{48,40},{56,48},{64,56},{72,6... | collective-permute-start | bytes 49160 | tf_op jit(solution)/shard_map/ppermute | solution.py:19
  6.5 9.0 %copy-start.1 = (bf16[1,8,64,128]{3,2,1,0:T(8,128)(2,1)S(1)}, bf16[1,8,64,128]{3,2,1,0:T(8,128)(2,1)}, u32[]{:S(2)}) copy-start(bf16[1,8,64,128]{3,2,1,0:T(8,128)(2,1)} %param.6) | copy-start | bytes 393220
  7.5 8.9 %copy-start.2 = (bf16[3,3,128,128]{3,2,1,0:T(8,128)(2,1)S(1)}, bf16[3,3,128,128]{3,2,1,0:T(8,128)(2,1)}, u32[]{:S(2)}) copy-start(bf16[3,3,128,128]{3,2,1,0:T(8,128)(2,1)} %param.7) | copy-start | bytes 884740
  9.6 7.0 %collective-permute-start.2 = (bf16[1,10,1,128]{3,2,1,0:T(2,128)(2,1)S(1)}, bf16[1,10,1,128]{3,2,1,0:T(2,128)(2,1)S(1)}, u32[]{:S(2)}, u32[]{:S(2)}) collective-permute-start(bf16[1,10,1,128]{3,2,1,0:T(2,128)(2,1)S(1)} %get-tuple-element.48), channel_id=1, source_target_pairs={{0,1},{1,2},{2,3},{3,4},{4,5},{5,6},{6,7},{7,0},{8,9},{9,10},{10,1... | collective-permute-start | bytes 7688 | tf_op jit(solution)/shard_map/ppermute | solution.py:17
  13.5 6.5 %collective-permute-start.3 = (bf16[1,10,1,128]{3,2,1,0:T(2,128)(2,1)S(1)}, bf16[1,10,1,128]{3,2,1,0:T(2,128)(2,1)S(1)}, u32[]{:S(2)}, u32[]{:S(2)}) collective-permute-start(bf16[1,10,1,128]{3,2,1,0:T(2,128)(2,1)S(1)} %get-tuple-element.49), channel_id=1, source_target_pairs={{1,0},{2,1},{3,2},{4,3},{5,4},{6,5},{7,6},{0,7},{9,8},{10,9},{11,1... | collective-permute-start | bytes 7688 | tf_op jit(solution)/shard_map/ppermute | solution.py:19
  22.5 29.5 %all-to-all-start = ((bf16[1,8,64,128]{3,1,0,2:T(8,128)(2,1)}), bf16[1,8,64,128]{3,1,0,2:T(8,128)(2,1)S(1)}, u32[]{:S(2)}, u32[]{:S(2)}) async-start(bf16[1,8,64,128]{3,1,0,2:T(8,128)(2,1)} %copy.21), calls=%async_computation | async-start | bytes 262144 | tf_op jit(solution)/shard_map/all_to_all | solution.py:90
  74.8 0.8 copy-start.3
where the time goes:
time: 76.9 us; the launch traced here: 76.4 us
  starting transfers between devices  28.2 us (37%)
  waiting for transfers between devices  18.1 us (24%)
  blocking collectives  16.8 us (22%)
  matrix products  6.15 us (8%)
  local copies, waits for them, and re-layouts  4.16 us (5%)
  other arithmetic  2.67 us (3%)
    all_to_all x1, blocking collectives, return_cells(): return lax.all_to_all(block, 'gx', split_axis=1, concat_axis=2, tiled=True)  16.8 us
    all_to_all x1, starting transfers between devices, on_device(): lax.all_to_all(normed, 'gx', split_axis=2, concat_axis=1, tiled=True)  16.7 us
    all_to_all x1, waiting for transfers between devices, on_device(): lax.all_to_all(normed, 'gx', split_axis=2, concat_axis=1, tiled=True)  12.8 us
    ppermute x2, starting transfers between devices, padded_2(): lax.ppermute(tail, axis, [(i, (i + 1) % count) for i in range(count)])  7.67 us
    ppermute x2, waiting for transfers between devices, padded_2(): lax.ppermute(head, axis, [((i + 1) % count, i) for i in range(count)])  5.32 us
    ppermute x2, starting transfers between devices, padded_2(): lax.ppermute(head, axis, [((i + 1) % count, i) for i in range(count)])  3.84 us
    unnamed x14, local copies, waits for them, and re-layouts  2.42 us
    dot_general x9, matrix products, convolve(): jnp.dot(window.reshape(-1, width), conv_weight[a, b], preferred_element_t...  2.4 us
  transfers between devices with their start and end apart: 5, of which 3 were waited for; matrix products, arithmetic and copies ran while one was open for 3% of the time, Pallas kernels for 0%

commit v1 on v0

--- a/solution.py
+++ b/solution.py
@@ -87,7 +87,13 @@
     normed = normalize(stem)
     attended = return_cells(
         attend_lines(
-            lax.all_to_all(normed, "gx", split_axis=2, concat_axis=1, tiled=True), qkv_weight
+            jnp.concatenate(
+                lax.all_to_all(
+                    jnp.stack(jnp.split(normed, lax.axis_size("gx"), axis=2)), "gx", 0, 0
+                ),
+                axis=1,
+            ),
+            qkv_weight,
         )
     )
     return finish(stem, attended, out_weight)

time: 76.9 us -> 114 us (1.48)
  local copies, waits for them, and re-layouts: 4.16 us -> 40.7 us
    unnamed x14 -> x77, local copies, waits for them, and re-layouts: 2.42 us -> 38.9 us
  transfers between devices with their start and end apart: 5 -> 5, of which waited for: 3 -> 3; matrix products, arithmetic and copies ran while one was open for 3% -> 2% of each run, Pallas kernels for 0% -> 0%
where the time goes in v1:
time: 114 us; the launch traced here: 113 us
  local copies, waits for them, and re-layouts  40.7 us (36%)
  starting transfers between devices  28.2 us (25%)
  waiting for transfers between devices  18.1 us (16%)
  blocking collectives  16.9 us (15%)
  matrix products  6.14 us (5%)
  other arithmetic  2.67 us (2%)
    unnamed x77, local copies, waits for them, and re-layouts  38.9 us
    all_to_all x1, blocking collectives, return_cells(): return lax.all_to_all(block, 'gx', split_axis=1, concat_axis=2, tiled=True)  16.9 us
    all_to_all x1, starting transfers between devices, on_device(): lax.all_to_all(jnp.stack(jnp.split(normed, lax.axis_size('gx'), axis=2)),...  16.7 us
    all_to_all x1, waiting for transfers between devices, on_device(): lax.all_to_all(jnp.stack(jnp.split(normed, lax.axis_size('gx'), axis=2)),...  12.8 us
    ppermute x2, starting transfers between devices, padded_2(): lax.ppermute(tail, axis, [(i, (i + 1) % count) for i in range(count)])  7.67 us
    ppermute x2, waiting for transfers between devices, padded_2(): lax.ppermute(head, axis, [((i + 1) % count, i) for i in range(count)])  5.32 us
    ppermute x2, starting transfers between devices, padded_2(): lax.ppermute(head, axis, [((i + 1) % count, i) for i in range(count)])  3.84 us
    dot_general x9, matrix products, convolve(): jnp.dot(window.reshape(-1, width), conv_weight[a, b], preferred_element_t...  2.4 us
  transfers between devices with their start and end apart: 5, of which 3 were waited for; matrix products, arithmetic and copies ran while one was open for 2% of the time, Pallas kernels for 0%

profile of v1, /device:TPU:7, one launch (start us, length us, event | category | flops | bytes accessed | tf_op | source)
XLA Modules:
  0.0 113.1 jit_solution(4138467299828289453)
XLA Ops:
  0.0 0.8 fusion.82
  0.8 3.8 %collective-permute-start = (bf16[1,1,64,128]{3,2,1,0:T(8,128)(2,1)S(1)}, bf16[1,1,64,128]{3,2,1,0:T(8,128)(2,1)S(1)}, u32[]{:S(2)}, u32[]{:S(2)}) collective-permute-start(bf16[1,1,64,128]{3,2,1,0:T(8,128)(2,1)S(1)} %get-tuple-element.125), channel_id=1, source_target_pairs={{0,8},{8,16},{16,24},{24,32},{32,40},{40,48},{48,56},{56,64},{64,7... | collective-permute-start | bytes 49160 | tf_op jit(solution)/shard_map/ppermute | solution.py:17
  4.5 1.9 %collective-permute-start.1 = (bf16[1,1,64,128]{3,2,1,0:T(8,128)(2,1)S(1)}, bf16[1,1,64,128]{3,2,1,0:T(8,128)(2,1)S(1)}, u32[]{:S(2)}, u32[]{:S(2)}) collective-permute-start(bf16[1,1,64,128]{3,2,1,0:T(8,128)(2,1)S(1)} %get-tuple-element.124), channel_id=1, source_target_pairs={{8,0},{16,8},{24,16},{32,24},{40,32},{48,40},{56,48},{64,56},{72,6... | collective-permute-start | bytes 49160 | tf_op jit(solution)/shard_map/ppermute | solution.py:19
  6.5 1.0 constant_dynamic-update-slice_fusion.1
  7.5 2.1 %collective-permute-done.1 = bf16[1,1,64,128]{3,2,1,0:T(8,128)(2,1)S(1)} collective-permute-done((bf16[1,1,64,128]{3,2,1,0:T(8,128)(2,1)S(1)}, bf16[1,1,64,128]{3,2,1,0:T(8,128)(2,1)S(1)}, u32[]{:S(2)}, u32[]{:S(2)}) %collective-permute-start.1) | collective-permute-done | bytes 16416 | tf_op jit(solution)/shard_map/ppermute | solution.py:19
  9.6 3.9 %collective-permute-start.2 = (bf16[1,10,1,128]{3,2,1,0:T(2,128)(2,1)S(1)}, bf16[1,10,1,128]{3,2,1,0:T(2,128)(2,1)S(1)}, u32[]{:S(2)}, u32[]{:S(2)}) collective-permute-start(bf16[1,10,1,128]{3,2,1,0:T(2,128)(2,1)S(1)} %get-tuple-element.58), channel_id=1, source_target_pairs={{0,1},{1,2},{2,3},{3,4},{4,5},{5,6},{6,7},{7,0},{8,9},{9,10},{10,1... | collective-permute-start | bytes 7688 | tf_op jit(solution)/shard_map/ppermute | solution.py:17
  13.5 1.9 %collective-permute-start.3 = (bf16[1,10,1,128]{3,2,1,0:T(2,128)(2,1)S(1)}, bf16[1,10,1,128]{3,2,1,0:T(2,128)(2,1)S(1)}, u32[]{:S(2)}, u32[]{:S(2)}) collective-permute-start(bf16[1,10,1,128]{3,2,1,0:T(2,128)(2,1)S(1)} %get-tuple-element.59), channel_id=1, source_target_pairs={{1,0},{2,1},{3,2},{4,3},{5,4},{6,5},{7,6},{0,7},{9,8},{10,9},{11,1... | collective-permute-start | bytes 7688 | tf_op jit(solution)/shard_map/ppermute | solution.py:19
  15.5 0.9 fusion.40
  16.8 3.2 %collective-permute-done.3 = bf16[1,10,1,128]{3,2,1,0:T(2,128)(2,1)S(1)} collective-permute-done((bf16[1,10,1,128]{3,2,1,0:T(2,128)(2,1)S(1)}, bf16[1,10,1,128]{3,2,1,0:T(2,128)(2,1)S(1)}, u32[]{:S(2)}, u32[]{:S(2)}) %collective-permute-start.3) | collective-permute-done | bytes 2592 | tf_op jit(solution)/shard_map/ppermute | solution.py:19
  22.0 0.6 constant_dynamic-update-slice_fusion.66
  22.6 0.6 constant_dynamic-update-slice_fusion.65
  23.1 0.6 constant_dynamic-update-slice_fusion.64
  23.7 0.6 constant_dynamic-update-slice_fusion.63
  24.3 0.6 constant_dynamic-update-slice_fusion.62
  24.9 0.6 constant_dynamic-update-slice_fusion.61
  25.5 0.6 constant_dynamic-update-slice_fusion.60
  26.0 0.6 constant_dynamic-update-slice_fusion.59
  26.6 0.6 constant_dynamic-update-slice_fusion.58
  27.2 0.6 constant_dynamic-update-slice_fusion.57
  27.8 0.6 constant_dynamic-update-slice_fusion.56
  28.4 0.6 constant_dynamic-update-slice_fusion.55
  28.9 0.6 constant_dynamic-update-slice_fusion.54
  29.5 0.6 constant_dynamic-update-slice_fusion.53
  30.1 0.6 constant_dynamic-update-slice_fusion.52
  30.7 0.6 constant_dynamic-update-slice_fusion.51
  59.1 16.7 %all-to-all-start = ((bf16[64,1,8,1,128]{4,2,3,1,0:T(8,128)(2,1)}), bf16[64,1,8,1,128]{4,2,3,1,0:T(8,128)(2,1)S(1)}, u32[]{:S(2)}, u32[]{:S(2)}) async-start(bf16[64,1,8,1,128]{4,2,3,1,0:T(8,128)(2,1)} %constant_dynamic-update-slice_fusion.3), calls=%async_computation | async-start | bytes 262144 | tf_op jit(solution)/shard_map/all_to_all | solution.py:91
  75.8 12.8 %all-to-all-done = bf16[64,1,8,1,128]{4,2,3,1,0:T(8,128)(2,1)S(1)} async-done(((bf16[64,1,8,1,128]{4,2,3,1,0:T(8,128)(2,1)}), bf16[64,1,8,1,128]{4,2,3,1,0:T(8,128)(2,1)S(1)}, u32[]{:S(2)}, u32[]{:S(2)}) %all-to-all-start) | async-done | bytes 131104 | tf_op jit(solution)/shard_map/all_to_all | solution.py:91
  88.9 3.4 %while.10 = (s32[]{:T(128)}, bf16[4,1,512,1,32]{2,4,3,1,0:T(8,128)(2,1)S(1)}, bf16[4,1,512,1,32]{2,4,3,1,0:T(8,128)(2,1)S(1)}, bf16[4,1,512,1,32]{2,4,3,1,0:T(8,...) while((s32[]{:T(128)}, bf16[4,1,512,1,32]{2,4,3,1,0:T(8,128)(2,1)S(1)}, ...), condition=%wide.region_5.6_spmd, body=%wide.region_2.5_spmd.sunk | while | flops 35404800 | bytes 3289157 | solution.py:49
  93.0 1.4 %reduce.8 = bf16[512,128]{1,0:T(8,128)(2,1)S(1)} reduce(bf16[512,1,1,128]{3,2,1,0:T(2,128)(2,1)S(1)} %bitcast.276, bf16[]{:T(256)} %broadcast.39), dimensions={1,2}, to_apply=%bitcast.256.reduce_sub_computation | reduce | bytes 262146
  94.5 16.9 %all_to_all.20 = bf16[64,2,512]{2,1,0:T(2,128)(2,1)S(1)} all-to-all(bf16[64,2,512]{2,1,0:T(2,128)(2,1)S(1)} %reshape.149), channel_id=1, replica_groups=mesh['gx'=64,'gy'=8] {'gx'}, dimensions={0} | all-to-all | bytes 262144 | tf_op jit(solution)/shard_map/all_to_all | solution.py:54
  111.5 0.7 copy-done.3
  112.2 0.8 fusion.15
  (96 shorter events, 34.6 us)
Async XLA Ops:
  0.0 88.6 %copy-start = (bf16[128,384]{1,0:T(8,128)(2,1)S(1)}, bf16[128,384]{1,0:T(8,128)(2,1)}, u32[]{:S(2)}) copy-start(bf16[128,384]{1,0:T(8,128)(2,1)} %param.8) | copy-start | bytes 294916
  0.8 5.7 %collective-permute-start = (bf16[1,1,64,128]{3,2,1,0:T(8,128)(2,1)S(1)}, bf16[1,1,64,128]{3,2,1,0:T(8,128)(2,1)S(1)}, u32[]{:S(2)}, u32[]{:S(2)}) collective-permute-start(bf16[1,1,64,128]{3,2,1,0:T(8,128)(2,1)S(1)} %get-tuple-element.125), channel_id=1, source_target_pairs={{0,8},{8,16},{16,24},{24,32},{32,40},{40,48},{48,56},{56,64},{64,7... | collective-permute-start | bytes 49160 | tf_op jit(solution)/shard_map/ppermute | solution.py:17
  4.5 5.1 %collective-permute-start.1 = (bf16[1,1,64,128]{3,2,1,0:T(8,128)(2,1)S(1)}, bf16[1,1,64,128]{3,2,1,0:T(8,128)(2,1)S(1)}, u32[]{:S(2)}, u32[]{:S(2)}) collective-permute-start(bf16[1,1,64,128]{3,2,1,0:T(8,128)(2,1)S(1)} %get-tuple-element.124), channel_id=1, source_target_pairs={{8,0},{16,8},{24,16},{32,24},{40,32},{48,40},{56,48},{64,56},{72,6... | collective-permute-start | bytes 49160 | tf_op jit(solution)/shard_map/ppermute | solution.py:19
  6.5 9.0 %copy-start.1 = (bf16[1,8,64,128]{3,2,1,0:T(8,128)(2,1)S(1)}, bf16[1,8,64,128]{3,2,1,0:T(8,128)(2,1)}, u32[]{:S(2)}) copy-start(bf16[1,8,64,128]{3,2,1,0:T(8,128)(2,1)} %param.6) | copy-start | bytes 393220
  7.5 8.9 %copy-start.2 = (bf16[3,3,128,128]{3,2,1,0:T(8,128)(2,1)S(1)}, bf16[3,3,128,128]{3,2,1,0:T(8,128)(2,1)}, u32[]{:S(2)}) copy-start(bf16[3,3,128,128]{3,2,1,0:T(8,128)(2,1)} %param.7) | copy-start | bytes 884740
  9.6 7.0 %collective-permute-start.2 = (bf16[1,10,1,128]{3,2,1,0:T(2,128)(2,1)S(1)}, bf16[1,10,1,128]{3,2,1,0:T(2,128)(2,1)S(1)}, u32[]{:S(2)}, u32[]{:S(2)}) collective-permute-start(bf16[1,10,1,128]{3,2,1,0:T(2,128)(2,1)S(1)} %get-tuple-element.58), channel_id=1, source_target_pairs={{0,1},{1,2},{2,3},{3,4},{4,5},{5,6},{6,7},{7,0},{8,9},{9,10},{10,1... | collective-permute-start | bytes 7688 | tf_op jit(solution)/shard_map/ppermute | solution.py:17
  13.5 6.5 %collective-permute-start.3 = (bf16[1,10,1,128]{3,2,1,0:T(2,128)(2,1)S(1)}, bf16[1,10,1,128]{3,2,1,0:T(2,128)(2,1)S(1)}, u32[]{:S(2)}, u32[]{:S(2)}) collective-permute-start(bf16[1,10,1,128]{3,2,1,0:T(2,128)(2,1)S(1)} %get-tuple-element.59), channel_id=1, source_target_pairs={{1,0},{2,1},{3,2},{4,3},{5,4},{6,5},{7,6},{0,7},{9,8},{10,9},{11,1... | collective-permute-start | bytes 7688 | tf_op jit(solution)/shard_map/ppermute | solution.py:19
  59.1 29.5 %all-to-all-start = ((bf16[64,1,8,1,128]{4,2,3,1,0:T(8,128)(2,1)}), bf16[64,1,8,1,128]{4,2,3,1,0:T(8,128)(2,1)S(1)}, u32[]{:S(2)}, u32[]{:S(2)}) async-start(bf16[64,1,8,1,128]{4,2,3,1,0:T(8,128)(2,1)} %constant_dynamic-update-slice_fusion.3), calls=%async_computation | async-start | bytes 262144 | tf_op jit(solution)/shard_map/all_to_all | solution.py:91
  111.5 0.8 copy-start.3
